TPU v7x, 32 devices: a whole 2x2x4 slice. The times are simulated.
32 devices in a mesh: task: 4 (over x, core), dp: 8 (over z, y).
Axes of the slice: x: 2, y: 2, z: 4, core: 2. Of those that a mesh axis runs over, the one named last changes fastest.
Arguments:
- inputs: bfloat16 [4, 2, 4096, 1024], P('task', None, 'dp'), may hold values from -48 to 48
- labels: int32 [4, 2, 4096], P('task', None, 'dp'), may hold values from 0 to 999
- w_hidden: float32 [4, 1024, 1024], P('task', 'dp'), may hold values from -6 to 6
- w_out: float32 [4, 1024, 1000], P('task', 'dp'), may hold values from -12 to 12
- mom_hidden: float32 [4, 1024, 1024], P('task', 'dp'), may hold values from -0.6 to 0.6
- mom_out: float32 [4, 1024, 1000], P('task', 'dp'), may hold values from -0.6 to 0.6
- signs: int32 [4], P('task'), may hold values from -1 to 1, as said below
- perturb: float32 [4, 512, 512], P('task', 'dp'), may hold values from -6 to 6
- hyper_in: float32 [8, 512], replicated, may hold values from -2 to 2
- hyper_mid: float32 [512, 512], P('dp'), may hold values from -0.25 to 0.25
- hyper_out: float32 [512, 21], replicated, may hold values from -0.25 to 0.25
Outputs:
- new_hidden: float32 [4, 1024, 1024], P('task', 'dp')
- new_out: float32 [4, 1024, 1000], P('task', 'dp')
- new_mom_hidden: float32 [4, 1024, 1024], P('task', 'dp')
- new_mom_out: float32 [4, 1024, 1000], P('task', 'dp')
- task_losses: float32 [4, 2], P('task')
- meta_grad: float32 [512, 512], P('dp')
Inputs may be any that keep to these rules, and one draw needn't show every extreme that they name: `signs`: each entry is +1 or -1.
All inputs are finite; a program needn't handle non-finite values.
Results may differ from a plain program's by a relative error of at most 0.01045.
The roundings to bfloat16 on the way count: a program that leaves them out, or rounds other values in their place, can miss the bound.
Values may be sent and summed in bfloat16 or wider, within the bound.
A program may use at most 128 MiB of HBM per device.

v0:
```python
import jax
import jax.numpy as jnp
from jax import lax
from jax.sharding import PartitionSpec as P

BETA = 0.8
FLOOR = 0.001
SIGMA = 0.01
LR_BASE = 0.03
HIGH = lax.Precision.HIGHEST
BY_ROWS = (((0,), (0,)), ((), ()))
BY_COLUMNS = (((1,), (1,)), ((), ()))


def moment_sums(gradient, moment, tensor):
    return jnp.stack(
        [
            jnp.sum(gradient * gradient),
            jnp.sum(moment * moment),
            jnp.sum(tensor * tensor),
            jnp.sum(gradient * moment),
        ]
    )


def tensor_inputs(sums, step, steps):
    grad_sq = sums[:, 0]
    moment_sq = sums[:, 1]
    weight_sq = sums[:, 2]
    cross_term = sums[:, 3]
    kind_table = jnp.eye(2, dtype=jnp.float32)
    step_share = jnp.full((2,), (step + 1.0) / steps, jnp.float32)
    return jnp.stack(
        [
            jnp.log(FLOOR + grad_sq),
            jnp.log(FLOOR + moment_sq),
            jnp.log(1.0 + weight_sq),
            cross_term / jnp.sqrt((FLOOR + grad_sq) * (FLOOR + moment_sq)),
            step_share,
            jnp.ones((2,), jnp.float32),
            kind_table[:, 0],
            kind_table[:, 1],
        ],
        axis=1,
    )


def apply_rule(tensor, gradient, moment, sums_row, coeffs):
    neurons = (coeffs.shape[0] - 1) // 5
    feat_grad = gradient / jnp.sqrt(FLOOR + sums_row[0])
    feat_moment = moment / jnp.sqrt(FLOOR + sums_row[1])
    direction = jnp.zeros_like(tensor)
    for neuron in range(neurons):
        inner = (
            coeffs[3 * neuron] * feat_grad
            + coeffs[3 * neuron + 1] * feat_moment
            + coeffs[3 * neuron + 2] * tensor
            + coeffs[3 * neurons + neuron]
        )
        direction = direction + coeffs[4 * neurons + neuron] * jnp.maximum(inner, 0.0)
    return tensor - LR_BASE * jnp.exp(coeffs[5 * neurons]) * direction


def on_device(
    inputs,
    labels,
    w_hidden,
    w_out,
    mom_hidden,
    mom_out,
    signs,
    perturb,
    hyper_in,
    hyper_mid,
    hyper_out,
):
    groups = lax.axis_size("dp")
    tasks = lax.axis_size("task")
    features = inputs[0]
    classes = labels[0]
    hidden_w = w_hidden[0]
    out_w = w_out[0]
    hidden_m = mom_hidden[0]
    out_m = mom_out[0]
    sign = signs[0].astype(jnp.float32)
    noise = perturb[0]
    own_rows = hyper_mid + SIGMA * sign * noise
    row_count = own_rows.shape[0]
    row_start = lax.axis_index("dp") * row_count
    steps = features.shape[0]
    local_batch = features.shape[1]
    width_in = features.shape[2]
    width_hidden = hidden_w.shape[1]
    class_count = out_w.shape[1]
    batch_total = local_batch * groups
    count_hidden = hidden_w.shape[0] * groups * width_hidden
    count_out = out_w.shape[0] * groups * class_count
    losses = []
    for step in range(steps):
        batch_in = features[step]
        hidden_b = hidden_w.astype(jnp.bfloat16)
        out_b = out_w.astype(jnp.bfloat16)
        before = jnp.dot(
            batch_in,
            lax.all_gather(hidden_b, "dp", axis=0, tiled=True),
            preferred_element_type=jnp.float32,
        ) * width_in ** (-0.5)
        active = jnp.maximum(before, 0.0).astype(jnp.bfloat16)
        logits = jnp.dot(
            active,
            lax.all_gather(out_b, "dp", axis=0, tiled=True),
            preferred_element_type=jnp.float32,
        ) * width_hidden ** (-0.5)
        shifted = logits - jnp.max(logits, axis=1, keepdims=True)
        log_total = jnp.log(jnp.sum(jnp.exp(shifted), axis=1, keepdims=True))
        onehot = (
            classes[step][:, None] == jnp.arange(class_count, dtype=jnp.int32)[None, :]
        ).astype(jnp.float32)
        example_loss = log_total[:, 0] - jnp.sum(shifted * onehot, axis=1)
        errors = (jnp.exp(shifted - log_total) - onehot).astype(jnp.bfloat16)
        grad_out = lax.psum_scatter(
            lax.dot_general(active, errors, BY_ROWS, preferred_element_type=jnp.float32),
            "dp",
            scatter_dimension=0,
            tiled=True,
        )
        grad_out = grad_out * width_hidden ** (-0.5)
        back = lax.dot_general(
            errors,
            lax.all_gather(out_b, "dp", axis=0, tiled=True),
            BY_COLUMNS,
            preferred_element_type=jnp.float32,
        )
        back = back * width_hidden ** (-0.5)
        back_pre = jnp.where(before > 0, back, 0.0).astype(jnp.bfloat16)
        grad_hidden = lax.psum_scatter(
            lax.dot_general(batch_in, back_pre, BY_ROWS, preferred_element_type=jnp.float32),
            "dp",
            scatter_dimension=0,
            tiled=True,
        ) * width_in ** (-0.5)
        hidden_m = BETA * hidden_m + (1.0 - BETA) * grad_hidden
        out_m = BETA * out_m + (1.0 - BETA) * grad_out
        local_sums = jnp.stack(
            [moment_sums(grad_hidden, hidden_m, hidden_w), moment_sums(grad_out, out_m, out_w)]
        )
        total_sums, loss_total = lax.psum((local_sums, jnp.sum(example_loss)), "dp")
        losses.append(loss_total / batch_total)
        sums = jnp.stack([total_sums[0] / count_hidden, total_sums[1] / count_out])
        opening = jnp.tanh(jnp.dot(tensor_inputs(sums, step, steps), hyper_in, precision=HIGH))
        share = jnp.dot(
            lax.dynamic_slice_in_dim(opening, row_start, row_count, 1), own_rows, precision=HIGH
        )
        middle = jnp.tanh(lax.psum(share, "dp"))
        coeffs = jnp.dot(middle, hyper_out, precision=HIGH)
        hidden_w = apply_rule(hidden_w, grad_hidden, hidden_m, sums[0], coeffs[0])
        out_w = apply_rule(out_w, grad_out, out_m, sums[1], coeffs[1])
    loss_row = jnp.stack(losses)
    score = jnp.sum(loss_row) / steps
    weighted, signed, total = lax.psum((sign * score * noise, sign * noise, score), "task")
    center = total / tasks
    meta_grad = (weighted - center * signed) / (SIGMA * tasks)
    return (hidden_w[None], out_w[None], hidden_m[None], out_m[None], loss_row[None, :], meta_grad)


def solution(mesh):
    in_specs = (
        P("task", None, "dp", None),
        P("task", None, "dp"),
        P("task", "dp", None),
        P("task", "dp", None),
        P("task", "dp", None),
        P("task", "dp", None),
        P("task"),
        P("task", "dp", None),
        P(),
        P("dp", None),
        P(),
    )
    out_specs = (
        P("task", "dp", None),
        P("task", "dp", None),
        P("task", "dp", None),
        P("task", "dp", None),
        P("task", None),
        P("dp", None),
    )
    return jax.shard_map(
        on_device, mesh=mesh, in_specs=in_specs, out_specs=out_specs, check_vma=False
    )
```

profile of v0, /device:TPU:0, one launch (start us, length us, event | category | flops | bytes accessed | tf_op | source)
XLA Modules:
  0.0 744.2 jit_solution(12231159281668797453)
XLA Ops:
  7.2 1.3 copy.17
  8.5 0.7 bitcast_convert_fusion
  9.4 0.7 bitcast_convert_fusion.1
  10.2 53.6 %all-gather.5.cloned.1.call-done = bf16[1024,1024]{0,1:T(8,128)(2,1)} async-done(((bf16[128,1024]{0,1:T(8,128)(2,1)}), bf16[1024,1024]{0,1:T(8,128)(2,1)}) %all-gather.5.cloned.1.call-update) | async-done | bytes 2097168 | tf_op jit(solution)/shard_map/all_gather | solution.py:105
  63.7 4.6 fusion.4
  68.3 46.0 %all-gather.7.cloned.1.call-done = bf16[1024,1000]{0,1:T(8,128)(2,1)} async-done(((bf16[128,1000]{0,1:T(8,128)(2,1)}), bf16[1024,1000]{0,1:T(8,128)(2,1)}) %all-gather.7.cloned.1.call-update) | async-done | bytes 2048016 | tf_op jit(solution)/shard_map/all_gather | solution.py:111
  114.3 3.6 multiply_reduce_fusion.1
  118.0 0.6 select_reduce_fusion.1
  118.6 0.6 subtract_reduce_fusion.1
  119.3 3.3 fusion.52
  122.7 7.6 %convolution_bitcast_fusion.1 = f32[1024,1024]{0,1:T(8,128)} fusion(f32[512,1024]{1,0:T(8,128)} %fusion.4, bf16[1024,1000]{0,1:T(8,128)(2,1)} %all-gather.7.cloned.1.call-done, bf16[1,2,512,1024]{3,2,1,0:T(8,128)(2,1)} %param.11, f32[512,1000]{0,1:T(8,128)} %copy-done.8, s32[512]{0:T(512)S(1)} %bitcast.298, f32[512]{0:T(512)S(1)} %get-tuple-element.46, ...), kind=kOutput, calls=%fused_computation.1 | convolution fusion | flops 2128523264 | bytes 11442176 | tf_op jit(solution)/shard_map/dot_general | solution.py:137
  130.4 0.9 copy-done.10
  131.3 0.2 copy.18
  132.2 0.8 fusion.31
  133.0 0.7 fusion.10
  133.8 72.4 %reduce-scatter.7.cloned.1.call-done = f32[128,1000]{0,1:T(8,128)} async-done(((f32[1024,1000]{0,1:T(8,128)}), f32[128,1000]{0,1:T(8,128)}) %reduce-scatter.7.cloned.1.call-update) | async-done | bytes 512016 | tf_op jit(solution)/shard_map/reduce_scatter | solution.py:121
  206.2 1.9 multiply_reduce_fusion.15
  208.1 89.7 %reduce-scatter.5.cloned.1.call-done = f32[128,1024]{0,1:T(8,128)} async-done(((f32[1024,1024]{0,1:T(8,128)}), f32[128,1024]{0,1:T(8,128)}) %reduce-scatter.5.cloned.1.call-update) | async-done | bytes 524304 | tf_op jit(solution)/shard_map/reduce_scatter | solution.py:136
  297.8 1.9 multiply_reduce_fusion.8
  299.7 5.2 maximum_bitcast_fusion
  304.9 20.1 %psum.63 = f32[2,4]{1,0:T(2,128)S(1)} all-reduce(f32[2,4]{1,0:T(2,128)S(1)} %pad_maximum_fusion), channel_id=1, replica_groups=mesh['task'=4,'dp'=8] {'dp'}, use_global_device_ids=true, to_apply=%region_12.13 | all-reduce | flops 8 | bytes 64 | tf_op jit(solution)/shard_map/psum | solution.py:147
  325.4 0.2 fusion.57
  325.6 17.1 %psum.64 = f32[2,512]{1,0:T(2,128)S(1)} all-reduce(f32[2,512]{1,0:T(2,128)S(1)} %fusion.57), channel_id=1, replica_groups=mesh['task'=4,'dp'=8] {'dp'}, use_global_device_ids=true, to_apply=%region_13.14 | all-reduce | flops 1024 | bytes 8192 | tf_op jit(solution)/shard_map/psum | solution.py:154
  342.7 0.1 fusion.60
  342.9 0.8 fusion.87
  343.6 0.7 fusion.88
  344.3 0.6 fusion.92
  346.9 13.7 %multiply_reduce_fusion.3 = (f32[]{:T(128)}, f32[128,1024]{0,1:T(8,128)S(1)}) fusion(f32[]{:T(128)} %bitcast.41, f32[]{:T(128)} %bitcast.40, f32[]{:T(128)} %bitcast.39, f32[]{:T(128)} %bitcast.38, f32[]{:T(128)} %bitcast.37, f32[]{:T(128)} %bitcast.36, f32[]{:T(128)} %bitcast.35, f32[]{:T(128)} %bitcast.34, f32[]{:T(128)} %bitcast.33, f32[]{:T(128)} %bitcast.32, ...), kind=kLoop, calls=%fused_computation.59 | loop fusion | flops 5505023 | bytes 2097248 | tf_op jit(solution)/shard_map/reduce_sum | solution.py:20
  360.6 0.7 convert_element_type.58
  361.4 0.7 fusion.86
  362.8 0.7 fusion.91
  364.9 14.8 %multiply_reduce_fusion.10 = (f32[]{:T(128)}, f32[128,1000]{0,1:T(8,128)S(1)}) fusion(f32[]{:T(128)} %bitcast.66, f32[]{:T(128)} %bitcast.65, f32[]{:T(128)} %bitcast.64, f32[]{:T(128)} %bitcast.63, f32[]{:T(128)} %bitcast.62, f32[]{:T(128)} %bitcast.61, f32[]{:T(128)} %bitcast.60, f32[]{:T(128)} %bitcast.59, f32[]{:T(128)} %bitcast.58, f32[]{:T(128)} %bitcast.57, ...), kind=kLoop, calls=%fused_computation.97 | loop fusion | flops 5375999 | bytes 2048096 | tf_op jit(solution)/shard_map/reduce_sum | solution.py:20
  379.7 0.7 convert_element_type.60
  380.4 0.2 reduce-scatter.11.cloned.1.call-start
  380.7 29.9 %all-gather.9.cloned.1.call-done = bf16[1024,1024]{0,1:T(8,128)(2,1)} async-done(((bf16[128,1024]{0,1:T(8,128)(2,1)}), bf16[1024,1024]{0,1:T(8,128)(2,1)}) %all-gather.9.cloned.1.call-update) | async-done | bytes 2097168 | tf_op jit(solution)/shard_map/all_gather | solution.py:105
  410.5 4.5 fusion.1
  415.0 45.9 %all-gather.11.cloned.1.call-done = bf16[1024,1000]{0,1:T(8,128)(2,1)} async-done(((bf16[128,1000]{0,1:T(8,128)(2,1)}), bf16[1024,1000]{0,1:T(8,128)(2,1)}) %all-gather.11.cloned.1.call-update) | async-done | bytes 2048016 | tf_op jit(solution)/shard_map/all_gather | solution.py:111
  461.0 3.6 multiply_reduce_fusion
  464.6 0.6 select_reduce_fusion
  465.2 0.6 subtract_reduce_fusion
  466.0 3.3 fusion.54
  469.3 7.6 %convolution_bitcast_fusion = f32[1024,1024]{0,1:T(8,128)} fusion(f32[1024,512]{0,1:T(8,128)} %fusion.1, bf16[1024,1000]{0,1:T(8,128)(2,1)} %all-gather.11.cloned.1.call-done, bf16[1,2,512,1024]{3,2,1,0:T(8,128)(2,1)} %param.11, f32[512,1000]{0,1:T(8,128)} %copy-done.7, s32[512]{0:T(512)S(1)} %bitcast.295, f32[512]{0:T(512)S(1)} %get-tuple-element.48, ...), kind=kOutput, calls=%fused_computation | convolution fusion | flops 2128523264 | bytes 11442176 | tf_op jit(solution)/shard_map/dot_general | solution.py:137
  477.0 75.7 %reduce-scatter.11.cloned.1.call-done = f32[128,1000]{0,1:T(8,128)} async-done(((f32[1024,1000]{0,1:T(8,128)}), f32[128,1000]{0,1:T(8,128)}) %reduce-scatter.11.cloned.1.call-update) | async-done | bytes 512016 | tf_op jit(solution)/shard_map/reduce_scatter | solution.py:121
  552.7 2.6 multiply_reduce_fusion.11
  555.3 2.7 maximum_bitcast_fusion.3
  558.0 86.6 %reduce-scatter.9.cloned.1.call-done = f32[128,1024]{0,1:T(8,128)} async-done(((f32[1024,1024]{0,1:T(8,128)}), f32[128,1024]{0,1:T(8,128)}) %reduce-scatter.9.cloned.1.call-update) | async-done | bytes 524304 | tf_op jit(solution)/shard_map/reduce_scatter | solution.py:136
  644.6 2.8 multiply_reduce_fusion.4
  647.3 2.7 maximum_bitcast_fusion.2
  650.1 20.1 %psum.65 = f32[2,4]{1,0:T(2,128)S(1)} all-reduce(f32[2,4]{1,0:T(2,128)S(1)} %pad_maximum_fusion.2), channel_id=1, replica_groups=mesh['task'=4,'dp'=8] {'dp'}, use_global_device_ids=true, to_apply=%region_26.27 | all-reduce | flops 8 | bytes 64 | tf_op jit(solution)/shard_map/psum | solution.py:147
  670.5 0.2 fusion.56
  670.7 18.0 %all-reduce = (f32[2,512]{1,0:T(2,128)S(1)}, f32[]{:T(128)}, f32[]{:T(128)}) all-reduce(f32[2,512]{1,0:T(2,128)S(1)} %fusion.56, f32[]{:T(128)} %get-tuple-element.47, f32[]{:T(128)} %get-tuple-element.45), channel_id=1, replica_groups=mesh['task'=4,'dp'=8] {'dp'}, use_global_device_ids=true, to_apply=%region_27.28 | all-reduce | flops 1026 | bytes 8208 | tf_op jit(solution)/shard_map/psum | solution.py:154
  688.9 0.8 fusion.83
  689.6 0.7 fusion.84
  690.4 0.6 fusion.89
  691.0 0.7 fusion.85
  691.6 0.6 fusion.90
  693.5 0.7 multiply_bitcast_fusion
  698.3 14.0 %subtract_bitcast_fusion = f32[1,128,1024]{1,2,0:T(8,128)} fusion(f32[128,1024]{0,1:T(8,128)S(1)} %get-tuple-element.34, f32[128,1024]{0,1:T(8,128)S(1)} %copy-done.2, f32[]{:T(128)} %bitcast.101, f32[]{:T(128)} %bitcast.100, f32[]{:T(128)} %bitcast.99, f32[]{:T(128)} %bitcast.98, f32[]{:T(128)} %bitcast.97, f32[]{:T(128)} %bitcast.96, f32[]{:T(128)} %bitcast.95, ...), kind=kLoop, calls=%fused_computation.57 | loop fusion | flops 5636096 | bytes 2097244 | tf_op jit(solution)/shard_map/broadcast_in_dim | solution.py:163
  712.3 14.3 %subtract_bitcast_fusion.1 = f32[1,128,1000]{1,2,0:T(8,128)} fusion(f32[128,1000]{0,1:T(8,128)S(1)} %get-tuple-element.36, f32[128,1000]{0,1:T(8,128)S(1)} %copy-done.6, f32[]{:T(128)} %bitcast.125, f32[]{:T(128)} %bitcast.124, f32[]{:T(128)} %bitcast.123, f32[]{:T(128)} %bitcast.122, f32[]{:T(128)} %bitcast.121, f32[]{:T(128)} %bitcast.120, f32[]{:T(128)} %bitcast.119, ...), kind=kLoop, calls=%fused_computation.95 | loop fusion | flops 5504000 | bytes 2048092 | tf_op jit(solution)/shard_map/broadcast_in_dim | solution.py:163
  726.6 6.1 psum.70
  732.8 1.0 copy.20
  733.8 1.0 copy.21
  735.4 0.6 maximum_bitcast_fusion.4
  736.0 1.6 subtract_multiply_fusion
  (69 shorter events, 1.7 us)
Async XLA Ops:
  7.2 335.6 %copy-start = (f32[512,21]{0,1:T(8,128)S(1)}, f32[512,21]{0,1:T(8,128)}, u32[]{:S(2)}) copy-start(f32[512,21]{0,1:T(8,128)} %param.21) | copy-start | bytes 129028
  7.2 2.2 copy-start.1
  7.2 3.0 copy-start.14
  7.2 56.5 %all-gather.5.cloned.1.call-start = ((), (), s32[]{:S(2)}) async-start(), calls=%async_computation.4 | async-start | bytes 2359296 | tf_op jit(solution)/shard_map/all_gather | solution.py:105
  9.3 105.0 %all-gather.7.cloned.1.call-start = ((), (), s32[]{:S(2)}) async-start(), calls=%async_computation.5 | async-start | bytes 2304000 | tf_op jit(solution)/shard_map/all_gather | solution.py:111
  10.1 196.1 %reduce-scatter.7.cloned.1.call-start = ((), (), s32[]{:S(2)}) async-start(), calls=%async_computation.7 | async-start | bytes 4608000 | tf_op jit(solution)/shard_map/reduce_scatter | solution.py:121
  114.3 5.0 copy-start.16
  118.0 1.4 copy-start.8
  122.6 175.2 %reduce-scatter.5.cloned.1.call-start = ((), (), s32[]{:S(2)}) async-start(), calls=%async_computation.6 | async-start | bytes 4718592 | tf_op jit(solution)/shard_map/reduce_scatter | solution.py:136
  130.3 1.0 copy-start.10
  130.3 75.9 %copy-start.12 = (f32[1,128,1000]{1,2,0:T(8,128)S(1)}, f32[1,128,1000]{1,2,0:T(8,128)}, u32[]{:S(2)}) copy-start(f32[1,128,1000]{1,2,0:T(8,128)} %param.16) | copy-start | bytes 1536004
  130.3 280.2 %all-gather.9.cloned.1.call-start = ((), (), s32[]{:S(2)}) async-start(), calls=%async_computation.8 | async-start | bytes 2359296 | tf_op jit(solution)/shard_map/all_gather | solution.py:105
  132.2 193.0 %copy-start.13 = (f32[8,512]{1,0:T(8,128)S(1)}, f32[8,512]{1,0:T(8,128)}, u32[]{:S(2)}) copy-start(f32[8,512]{1,0:T(8,128)} %param.19) | copy-start | bytes 49156
  132.2 193.1 %copy-start.9 = (f32[1,64,512]{2,1,0:T(8,128)S(1)}, f32[1,64,512]{2,1,0:T(8,128)}, u32[]{:S(2)}) copy-start(f32[1,64,512]{2,1,0:T(8,128)} %param.18) | copy-start | bytes 393220
  132.2 193.1 %copy-start.11 = (f32[64,512]{1,0:T(8,128)S(1)}, f32[64,512]{1,0:T(8,128)}, u32[]{:S(2)}) copy-start(f32[64,512]{1,0:T(8,128)} %param.20) | copy-start | bytes 393220
  297.8 49.0 %copy-start.5 = (f32[128,1024]{0,1:T(8,128)S(1)}, f32[128,1024]{0,1:T(8,128)}, u32[]{:S(2)}) copy-start(f32[128,1024]{0,1:T(8,128)} %reduce-scatter.5.cloned.1.call-done) | copy-start | bytes 1572868
  361.3 99.6 %all-gather.11.cloned.1.call-start = ((), (), s32[]{:S(2)}) async-start(), calls=%async_computation.9 | async-start | bytes 2304000 | tf_op jit(solution)/shard_map/all_gather | solution.py:111
  380.4 172.3 %reduce-scatter.11.cloned.1.call-start = ((), (), s32[]{:S(2)}) async-start(), calls=%async_computation.11 | async-start | bytes 4608000 | tf_op jit(solution)/shard_map/reduce_scatter | solution.py:121
  461.0 5.0 copy-start.15
  464.6 1.4 copy-start.7
  469.3 175.3 %reduce-scatter.9.cloned.1.call-start = ((), (), s32[]{:S(2)}) async-start(), calls=%async_computation.10 | async-start | bytes 4718592 | tf_op jit(solution)/shard_map/reduce_scatter | solution.py:136
  476.9 259.0 %all-reduce.4.cloned.1.call-start = ((), (), s32[]{:S(2)}) async-start(), calls=%async_computation.12 | async-start | bytes 524288 | tf_op jit(solution)/shard_map/psum | solution.py:160
  644.6 53.7 %copy-start.2 = (f32[128,1024]{0,1:T(8,128)S(1)}, f32[128,1024]{0,1:T(8,128)}, u32[]{:S(2)}) copy-start(f32[128,1024]{0,1:T(8,128)} %reduce-scatter.9.cloned.1.call-done) | copy-start | bytes 1572868
  647.3 65.0 %copy-start.6 = (f32[128,1000]{0,1:T(8,128)S(1)}, f32[128,1000]{0,1:T(8,128)}, u32[]{:S(2)}) copy-start(f32[128,1000]{0,1:T(8,128)} %reduce-scatter.11.cloned.1.call-done) | copy-start | bytes 1536004
  712.3 20.5 %copy-start.4 = (f32[1,128,1024]{1,2,0:T(8,128)S(1)}, f32[1,128,1024]{1,2,0:T(8,128)}, u32[]{:S(2)}) copy-start(f32[1,128,1024]{1,2,0:T(8,128)} %subtract_bitcast_fusion) | copy-start | bytes 1572868
  712.3 21.5 %copy-start.3 = (f32[1,128,1024]{1,2,0:T(8,128)S(1)}, f32[1,128,1024]{1,2,0:T(8,128)}, u32[]{:S(2)}) copy-start(f32[1,128,1024]{1,2,0:T(8,128)} %get-tuple-element.39) | copy-start | bytes 1572868
Sparse Core Ops, SparseCore 0:
  10.6 53.0 all-gather.4
  66.3 47.9 all-gather.6
  122.8 83.3 reduce-scatter.6
  209.6 88.1 reduce-scatter.4
  361.5 49.0 all-gather.8
  413.0 47.9 all-gather.10
  469.4 83.2 reduce-scatter.10
  556.4 88.1 reduce-scatter.8
  698.4 31.0 all-reduce.3
where the time goes:
time: 746 us; the launch traced here: 744 us
  waiting for transfers between devices  500 us (67%)
  other arithmetic  86.6 us (12%)
  blocking collectives  81.5 us (11%)
  matrix products  39.1 us (5%)
  between operations  24.7 us (3%)
  local copies, waits for them, and re-layouts  11.7 us (2%)
    reduce_scatter x2, waiting for transfers between devices, on_device(): lax.psum_scatter(lax.dot_general(batch_in, back_pre, BY_ROWS, preferred_e...  176 us
    reduce_scatter x2, waiting for transfers between devices, on_device(): lax.psum_scatter(lax.dot_general(active, errors, BY_ROWS, preferred_eleme...  148 us
    all_gather x2, waiting for transfers between devices, on_device(): lax.all_gather(out_b, 'dp', axis=0, tiled=True)  92 us
    all_gather x2, waiting for transfers between devices, on_device(): lax.all_gather(hidden_b, 'dp', axis=0, tiled=True)  83.4 us
    psum x2, blocking collectives, on_device(): total_sums, loss_total = lax.psum((local_sums, jnp.sum(example_loss)), 'dp')  40.2 us
    psum x2, blocking collectives, on_device(): middle = jnp.tanh(lax.psum(share, 'dp'))  35.2 us
    reduce_sum x4, other arithmetic, moment_sums(): jnp.sum(tensor * tensor)  30.1 us
    dot_general x2, matrix products, on_device(): lax.dot_general(batch_in, back_pre, BY_ROWS, preferred_element_type=jnp.f...  15.2 us
  transfers between devices with their start and end apart: 9, of which 8 were waited for; matrix products, arithmetic and copies ran while one was open for 11% of the time, Pallas kernels for 0%

commit v1 on v0

v1 whole, which is shorter than its diff:
```python
import functools

import jax
import jax.numpy as jnp
from jax import lax
from jax.experimental import pallas as pl
from jax.experimental.pallas import tpu as pltpu
from jax.sharding import PartitionSpec as P

BETA = 0.8
FLOOR = 0.001
SIGMA = 0.01
LR_BASE = 0.03
LANES = 128
HIGH = lax.Precision.HIGHEST
BY_ROWS = (((0,), (0,)), ((), ()))
BY_COLUMNS = (((1,), (1,)), ((), ()))
MESH = pl.DeviceIdType.MESH
F32 = jnp.float32
BF16 = jnp.bfloat16

HIDDEN_W, OUT_W, OUT_G, HIDDEN_G, STATS, SHARE = range(6)
NOISE, SCORE = range(2)


def fold(value):
    rows, columns = value.shape
    total = value[0:8]
    for row in range(8, rows, 8):
        total = total + value[row : row + 8]
    out = total[:, 0:LANES]
    for column in range(LANES, columns, LANES):
        out = out + total[:, column : column + LANES]
    return out


def full_sum(value):
    return jnp.sum(jnp.sum(value, axis=1, keepdims=True), axis=0, keepdims=True)


def kernel(
    n,
    tasks,
    x_ref,
    label_ref,
    w1_ref,
    w2_ref,
    m1_ref,
    m2_ref,
    sign_ref,
    noise_ref,
    hin_ref,
    mid_ref,
    hout_ref,
    p1,
    new_out,
    q1,
    new_mom_out,
    loss_ref,
    meta_ref,
    full1,
    full2,
    send1,
    send2,
    recv1,
    recv2,
    act,
    err,
    dpre,
    p2,
    q2,
    g1,
    g2,
    example,
    stat_send,
    stat_recv,
    share_send,
    share_recv,
    hout,
    losses,
    noise_send,
    noise_recv,
    score_send,
    score_recv,
    send_sem,
    recv_sem,
    task_send_sem,
    task_recv_sem,
):
    me = lax.axis_index("dp")
    task = lax.axis_index("task")
    steps, local_batch, width_in = x_ref.shape
    rows1 = w1_ref.shape[0]
    rows2, class_count = w2_ref.shape
    width_hidden = w1_ref.shape[1]
    padded = p2.shape[1]
    hyper_rows = mid_ref.shape[0]
    chunk = min(256, local_batch)
    block = min(256, width_hidden, width_in)
    scale_in = width_in ** (-0.5)
    scale_hidden = width_hidden ** (-0.5)
    batch_total = local_batch * n
    lane8 = lax.broadcasted_iota(jnp.int32, (8, LANES), 1)
    row8 = lax.broadcasted_iota(jnp.int32, (8, LANES), 0)

    barrier = pltpu.get_barrier_semaphore()

    @pl.loop(1, n)
    def _(k):
        pl.semaphore_signal(
            barrier, inc=1, device_id={"dp": lax.rem(me + k, n)}, device_id_type=MESH
        )

    @pl.loop(1, tasks)
    def _(k):
        pl.semaphore_signal(
            barrier, inc=1, device_id={"task": lax.rem(task + k, tasks)}, device_id_type=MESH
        )

    p1[...] = w1_ref[...]
    q1[...] = m1_ref[...]
    p2[...] = jnp.zeros_like(p2)
    q2[...] = jnp.zeros_like(q2)
    p2[:, 0:class_count] = w2_ref[...]
    q2[:, 0:class_count] = m2_ref[...]
    hout[...] = jnp.zeros_like(hout)
    hout[:, 0 : hout_ref.shape[1]] = hout_ref[...]
    noise_send[...] = noise_ref[...]
    pl.semaphore_wait(barrier, n - 1 + tasks - 1)

    def noise_copy(k):
        return pltpu.make_async_remote_copy(
            src_ref=noise_send,
            dst_ref=noise_recv.at[k],
            send_sem=task_send_sem.at[NOISE, k],
            recv_sem=task_recv_sem.at[NOISE, k],
            device_id={"task": lax.rem(task + k, tasks)},
            device_id_type=MESH,
        )

    def score_copy(k):
        return pltpu.make_async_remote_copy(
            src_ref=score_send,
            dst_ref=score_recv.at[k],
            send_sem=task_send_sem.at[SCORE, k],
            recv_sem=task_recv_sem.at[SCORE, k],
            device_id={"task": lax.rem(task + k, tasks)},
            device_id_type=MESH,
        )

    def one_step(step, carry):
        def copy(stage, k):
            peer = lax.rem(me + k, n)
            if stage == HIDDEN_W:
                own = full1.at[step, pl.ds(pl.multiple_of(me * rows1, rows1), rows1)]
                source, target = own, own
            elif stage == OUT_W:
                own = full2.at[step, pl.ds(pl.multiple_of(me * rows2, rows2), rows2)]
                source, target = own, own
            elif stage == OUT_G:
                source = send2.at[step, pl.ds(pl.multiple_of(peer * rows2, rows2), rows2)]
                target = recv2.at[step, k]
            elif stage == HIDDEN_G:
                source = send1.at[step, pl.ds(pl.multiple_of(peer * rows1, rows1), rows1)]
                target = recv1.at[step, k]
            elif stage == STATS:
                source, target = stat_send.at[step], stat_recv.at[step, k]
            else:
                source, target = share_send.at[step], share_recv.at[step, k]
            return pltpu.make_async_remote_copy(
                src_ref=source,
                dst_ref=target,
                send_sem=send_sem.at[step, stage, k],
                recv_sem=recv_sem.at[step, stage, k],
                device_id={"dp": peer},
                device_id_type=MESH,
            )

        def start(stage):
            @pl.loop(1, n)
            def _(k):
                copy(stage, k).start()

        def arrive(stage):
            @pl.loop(1, n)
            def _(k):
                copy(stage, k).wait_recv()

        full1[step, pl.ds(pl.multiple_of(me * rows1, rows1), rows1)] = p1[...].astype(BF16)
        full2[step, pl.ds(pl.multiple_of(me * rows2, rows2), rows2)] = p2[...].astype(BF16)
        start(HIDDEN_W)
        start(OUT_W)

        arrive(HIDDEN_W)

        @pl.loop(0, local_batch // chunk)
        def _(i):
            at = pl.ds(pl.multiple_of(i * chunk, chunk), chunk)
            pre = jnp.dot(x_ref[step, at, :], full1[step], preferred_element_type=F32)
            act[at, :] = jnp.maximum(pre * scale_in, 0.0).astype(BF16)

        arrive(OUT_W)

        @pl.loop(0, local_batch // chunk)
        def _(i):
            at = pl.ds(pl.multiple_of(i * chunk, chunk), chunk)
            logits = jnp.dot(act[at, :], full2[step], preferred_element_type=F32) * scale_hidden
            column = lax.broadcasted_iota(jnp.int32, logits.shape, 1)
            logits = jnp.where(column < class_count, logits, -jnp.inf)
            shifted = logits - jnp.max(logits, axis=1, keepdims=True)
            weight = jnp.exp(shifted)
            total = jnp.sum(weight, axis=1, keepdims=True)
            hit = column == label_ref[step, at, :]
            picked = jnp.sum(jnp.where(hit, shifted, 0.0), axis=1, keepdims=True)
            example[at, :] = jnp.log(total) - picked
            err[at, :] = (weight * (1.0 / total) - jnp.where(hit, 1.0, 0.0)).astype(BF16)

        @pl.loop(0, width_hidden // block)
        def _(i):
            at = pl.ds(pl.multiple_of(i * block, block), block)
            grad = lax.dot_general(act[:, at], err[...], BY_ROWS, preferred_element_type=F32)
            send2[step, at, :] = grad.astype(BF16)

        start(OUT_G)

        @pl.loop(0, local_batch // chunk)
        def _(i):
            at = pl.ds(pl.multiple_of(i * chunk, chunk), chunk)
            back = lax.dot_general(err[at, :], full2[step], BY_COLUMNS, preferred_element_type=F32)
            live = act[at, :].astype(F32) > 0.0
            dpre[at, :] = jnp.where(live, back * scale_hidden, 0.0).astype(BF16)

        @pl.loop(0, width_in // block)
        def _(i):
            at = pl.ds(pl.multiple_of(i * block, block), block)
            grad = lax.dot_general(x_ref[step, :, at], dpre[...], BY_ROWS, preferred_element_type=F32)
            send1[step, at, :] = grad.astype(BF16)

        start(HIDDEN_G)

        def reduce(sent, received, gradient, moment, tensor, rows, scale):
            def body(i, sums):
                offset = pl.multiple_of(i * 16, 16)
                at = pl.ds(offset, 16)
                own = pl.ds(pl.multiple_of(me * rows + offset, 16), 16)
                grad = sent[step, own, :].astype(F32)
                for k in range(1, n):
                    grad = grad + received[step, k, at, :].astype(F32)
                grad = grad * scale
                mom = BETA * moment[at, :] + (1.0 - BETA) * grad
                value = tensor[at, :]
                gradient[at, :] = grad
                moment[at, :] = mom
                return (
                    sums[0] + fold(grad * grad),
                    sums[1] + fold(mom * mom),
                    sums[2] + fold(value * value),
                    sums[3] + fold(grad * mom),
                )

            zero = jnp.zeros((8, LANES), F32)
            return lax.fori_loop(0, rows // 16, body, (zero, zero, zero, zero))

        arrive(OUT_G)
        sums2 = reduce(send2, recv2, g2, q2, p2, rows2, scale_hidden)
        arrive(HIDDEN_G)
        sums1 = reduce(send1, recv1, g1, q1, p1, rows1, scale_in)
        tile = jnp.zeros((8, LANES), F32)
        for row, sums in enumerate((sums1, sums2)):
            for lane, value in enumerate(sums):
                tile = tile + jnp.where((row8 == row) & (lane8 == lane), full_sum(value), 0.0)
        loss_sum = jnp.sum(example[...], axis=0, keepdims=True)
        tile = tile + jnp.where((row8 == 0) & (lane8 == 4), loss_sum, 0.0)
        stat_send[step] = tile
        start(STATS)
        arrive(STATS)
        for k in range(1, n):
            tile = tile + stat_recv[step, k]
        losses[step] = jnp.broadcast_to(tile[0:1, 4:5] / batch_total, (8, LANES))

        row_id = lax.broadcasted_iota(jnp.int32, (8, 1), 0)
        share_of = jnp.where(row_id == 0, 1.0 / (rows1 * n * width_hidden), 1.0 / (rows2 * n * class_count))
        means = tile * share_of
        a, b, c, e = (means[:, i : i + 1] for i in range(4))
        step_share = (step.astype(F32) + 1.0) / steps
        z = [
            jnp.log(FLOOR + a),
            jnp.log(FLOOR + b),
            jnp.log(1.0 + c),
            e / jnp.sqrt((FLOOR + a) * (FLOOR + b)),
            jnp.full((8, 1), step_share, F32),
            jnp.ones((8, 1), F32),
            jnp.where(row_id == 0, 1.0, 0.0),
            jnp.where(row_id == 1, 1.0, 0.0),
        ]
        own_in = jnp.zeros((hin_ref.shape[0], hyper_rows), F32)
        for i in range(n):
            part = hin_ref[:, i * hyper_rows : (i + 1) * hyper_rows]
            own_in = own_in + jnp.where(me == i, part, 0.0)
        mixed = jnp.zeros((8, hyper_rows), F32)
        for i in range(hin_ref.shape[0]):
            mixed = mixed + z[i] * own_in[i : i + 1, :]
        opening = jnp.tanh(mixed)
        theta = mid_ref[...] + SIGMA * sign_ref[...] * noise_ref[...]
        part = jnp.dot(opening, theta, precision=HIGH, preferred_element_type=F32)
        share_send[step] = part
        start(SHARE)
        arrive(SHARE)
        for k in range(1, n):
            part = part + share_recv[step, k]
        middle = jnp.tanh(part)
        gen = jnp.dot(middle, hout[...], precision=HIGH, preferred_element_type=F32)

        neurons = (hout_ref.shape[1] - 1) // 5

        def update(tensor, gradient, moment, row, limit):
            def number(j):
                return gen[row : row + 1, j : j + 1]

            def spread(value):
                return jnp.broadcast_to(value, (8, LANES))

            by_grad = lax.rsqrt(FLOOR + a[row : row + 1])
            by_moment = lax.rsqrt(FLOOR + b[row : row + 1])
            rate = LR_BASE * jnp.exp(number(5 * neurons))
            coeffs = []
            for j in range(neurons):
                coeffs.append(
                    (
                        spread(number(3 * j) * by_grad),
                        spread(number(3 * j + 1) * by_moment),
                        spread(number(3 * j + 2)),
                        spread(number(3 * neurons + j)),
                        spread(number(4 * neurons + j)),
                    )
                )
            rate = spread(rate)

            @pl.loop(0, tensor.shape[0] // 8)
            def _(i):
                at = pl.ds(pl.multiple_of(i * 8, 8), 8)
                for column in range(0, tensor.shape[1], LANES):
                    cols = slice(column, column + LANES)
                    grad = gradient[at, cols]
                    mom = moment[at, cols]
                    value = tensor[at, cols]
                    direction = jnp.zeros_like(value)
                    for by_g, by_m, by_p, bias, gain in coeffs:
                        inner = by_g * grad + by_m * mom + by_p * value + bias
                        direction = direction + gain * jnp.maximum(inner, 0.0)
                    value = value - rate * direction
                    if column + LANES > limit:
                        value = jnp.where(lane8 + column < limit, value, 0.0)
                    tensor[at, cols] = value

        update(p1, g1, q1, 0, width_hidden)
        update(p2, g2, q2, 1, class_count)

        for stage in range(6):

            @pl.loop(1, n)
            def _(k):
                copy(stage, k).wait_send()

        return carry

    @pl.loop(1, tasks)
    def _(k):
        noise_copy(k).start()

    lax.fori_loop(0, steps, one_step, 0)

    score = jnp.zeros((8, LANES), F32)
    row = jnp.zeros((8, LANES), F32)
    for s in range(steps):
        score = score + losses[s]
        row = row + jnp.where(lane8 == s, losses[s], 0.0)
    score = score / steps
    loss_ref[...] = row[0:1, 0:steps]
    sign = sign_ref[...]
    score_send[...] = jnp.where(row8 < 4, score, sign)

    @pl.loop(1, tasks)
    def _(k):
        score_copy(k).start()

    new_out[...] = p2[:, 0:class_count]
    new_mom_out[...] = q2[:, 0:class_count]

    @pl.loop(1, tasks)
    def _(k):
        score_copy(k).wait_recv()
        noise_copy(k).wait_recv()

    center = score[0:1, 0:1]
    for k in range(1, tasks):
        center = center + score_recv[k][0:1, 0:1]
    center = center / tasks
    meta = sign * (score[0:1, 0:1] - center) * noise_ref[...]
    for k in range(1, tasks):
        other = score_recv[k]
        meta = meta + other[4:5, 0:1] * (other[0:1, 0:1] - center) * noise_recv[k]
    meta_ref[...] = meta / (SIGMA * tasks)

    @pl.loop(1, tasks)
    def _(k):
        score_copy(k).wait_send()
        noise_copy(k).wait_send()


def on_device(
    inputs,
    labels,
    w_hidden,
    w_out,
    mom_hidden,
    mom_out,
    signs,
    perturb,
    hyper_in,
    hyper_mid,
    hyper_out,
):
    n = lax.axis_size("dp")
    tasks = lax.axis_size("task")
    steps, local_batch, width_in = inputs.shape[1:]
    rows1, width_hidden = w_hidden.shape[1:]
    rows2, class_count = w_out.shape[1:]
    hyper_rows, hyper = hyper_mid.shape
    padded = -(-class_count // LANES) * LANES
    gens = -(-hyper_out.shape[1] // LANES) * LANES
    vmem = pl.BlockSpec(memory_space=pltpu.VMEM)
    out_shape = (
        jax.ShapeDtypeStruct((rows1, width_hidden), F32),
        jax.ShapeDtypeStruct((rows2, class_count), F32),
        jax.ShapeDtypeStruct((rows1, width_hidden), F32),
        jax.ShapeDtypeStruct((rows2, class_count), F32),
        jax.ShapeDtypeStruct((1, steps), F32),
        jax.ShapeDtypeStruct((hyper_rows, hyper), F32),
    )
    scratch = [
        pltpu.VMEM((steps, rows1 * n, width_hidden), BF16),
        pltpu.VMEM((steps, rows2 * n, padded), BF16),
        pltpu.VMEM((steps, rows1 * n, width_hidden), BF16),
        pltpu.VMEM((steps, rows2 * n, padded), BF16),
        pltpu.VMEM((steps, n, rows1, width_hidden), BF16),
        pltpu.VMEM((steps, n, rows2, padded), BF16),
        pltpu.VMEM((local_batch, width_hidden), BF16),
        pltpu.VMEM((local_batch, padded), BF16),
        pltpu.VMEM((local_batch, width_hidden), BF16),
        pltpu.VMEM((rows2, padded), F32),
        pltpu.VMEM((rows2, padded), F32),
        pltpu.VMEM((rows1, width_hidden), F32),
        pltpu.VMEM((rows2, padded), F32),
        pltpu.VMEM((local_batch, 1), F32),
        pltpu.VMEM((steps, 8, LANES), F32),
        pltpu.VMEM((steps, n, 8, LANES), F32),
        pltpu.VMEM((steps, 8, hyper), F32),
        pltpu.VMEM((steps, n, 8, hyper), F32),
        pltpu.VMEM((hyper, gens), F32),
        pltpu.VMEM((steps, 8, LANES), F32),
        pltpu.VMEM((hyper_rows, hyper), F32),
        pltpu.VMEM((tasks, hyper_rows, hyper), F32),
        pltpu.VMEM((8, LANES), F32),
        pltpu.VMEM((tasks, 8, LANES), F32),
        pltpu.SemaphoreType.DMA((steps, 6, n)),
        pltpu.SemaphoreType.DMA((steps, 6, n)),
        pltpu.SemaphoreType.DMA((2, tasks)),
        pltpu.SemaphoreType.DMA((2, tasks)),
    ]
    outs = pl.pallas_call(
        functools.partial(kernel, n, tasks),
        out_shape=out_shape,
        in_specs=[vmem] * 11,
        out_specs=(vmem,) * 6,
        scratch_shapes=scratch,
        compiler_params=pltpu.CompilerParams(
            collective_id=0, has_side_effects=True, vmem_limit_bytes=60 * 1024 * 1024
        ),
    )(
        inputs[0],
        labels[0][:, :, None],
        w_hidden[0],
        w_out[0],
        mom_hidden[0],
        mom_out[0],
        signs.astype(F32)[:, None],
        perturb[0],
        hyper_in,
        hyper_mid,
        hyper_out,
    )
    return tuple(out[None] for out in outs[:4]) + (outs[4], outs[5])


def solution(mesh):
    in_specs = (
        P("task", None, "dp", None),
        P("task", None, "dp"),
        P("task", "dp", None),
        P("task", "dp", None),
        P("task", "dp", None),
        P("task", "dp", None),
        P("task"),
        P("task", "dp", None),
        P(),
        P("dp", None),
        P(),
    )
    out_specs = (
        P("task", "dp", None),
        P("task", "dp", None),
        P("task", "dp", None),
        P("task", "dp", None),
        P("task", None),
        P("dp", None),
    )
    return jax.shard_map(
        on_device, mesh=mesh, in_specs=in_specs, out_specs=out_specs, check_vma=False
    )
```

time: 746 us -> 433 us (0.58)
  waiting for transfers between devices: 500 us -> 0 us
  Pallas kernels: 0 us -> 418 us
  other arithmetic: 86.6 us -> 0 us
  blocking collectives: 81.5 us -> 0 us
  matrix products: 39.1 us -> 0 us
  between operations: 24.7 us -> 1.39 us
    pallas_call x0 -> x1, Pallas kernels: none -> 418 us  [on_device(): pl.pallas_call(functools.partial(kernel, n, tasks), out_shape=out_shape,...]
    reduce_scatter x4 -> x0, waiting for transfers between devices: 324 us -> none  [the longest x2 176 us: on_device(): lax.psum_scatter(lax.dot_general(batch_in, back_pre, BY_ROWS, preferred_e...]
    all_gather x4 -> x0, waiting for transfers between devices: 175 us -> none  [the longest x2 92 us: on_device(): lax.all_gather(out_b, 'dp', axis=0, tiled=True)]
    psum x5 -> x0, blocking collectives: 81.5 us -> none  [the longest x2 40.2 us: on_device(): total_sums, loss_total = lax.psum((local_sums, jnp.sum(example_loss)), 'dp')]
    reduce_sum x12 -> x0, other arithmetic: 41.6 us -> none  [the longest x4 30.1 us: moment_sums(): jnp.sum(tensor * tensor)]
    dot_general x14 -> x0, matrix products: 39.1 us -> none  [the longest x2 15.2 us: on_device(): lax.dot_general(batch_in, back_pre, BY_ROWS, preferred_element_type=jnp.f...]
    broadcast_in_dim x3 -> x0, other arithmetic: 28.9 us -> none  [the longest x1 14.3 us: on_device(): out_w[None]]
    another operation x7 -> x0, other arithmetic: 10.6 us -> none  [the longest x5 10.6 us: on_device(): jnp.stack([moment_sums(grad_hidden, hidden_m, hidden_w), moment_sums(grad...]
  transfers between devices with their start and end apart: 9 -> 0, of which waited for: 8 -> 0; matrix products, arithmetic and copies ran while one was open for 11% -> 0% of each run, Pallas kernels for 0% -> 0%
where the time goes in v1:
time: 433 us
  Pallas kernels  418 us (97%)
  local copies, waits for them, and re-layouts  13.3 us (3%)
    pallas_call x1, Pallas kernels, on_device(): pl.pallas_call(functools.partial(kernel, n, tasks), out_shape=out_shape,...  418 us
    unnamed x19, local copies, waits for them, and re-layouts  11.6 us

profile of v1, /device:TPU:0, one launch (start us, length us, event | category | flops | bytes accessed | tf_op | source)
XLA Modules:
  0.0 432.7 jit_solution(1944950601360911690)
XLA Ops:
  0.6 0.0 copy-start.2
  1.3 1.6 copy.25.hout_ref
  3.0 1.7 copy.24.label_ref
  4.7 2.0 copy.22
  6.7 0.0 copy-done.2
  6.7 1.0 copy.23
  7.7 418.0 %shard_map.154 = (f32[128,1024]{1,0:T(8,128)}, f32[128,1000]{1,0:T(8,128)}, f32[128,1024]{1,0:T(8,128)}, f32[128,1000]{1,0:T(8,128)}, f32[1,2]{1,0:T(1,128)}, /*index=5*/f32[64,512]{1,0:T(8,128)}) custom-call(bf16[2,512,1024]{2,1,0:T(8,128)(2,1)} %bitcast.12, s32[2,512,1]{2,1,0:T(8,128)} %copy.24.label_ref, f32[128,1024]{1,0:T(8,128)} %bitcast.19, ...), custom_call_target="tpu_custom_call" | custom-call | tf_op jit(solution)/shard_map/pallas_call | solution.py:471
  425.7 0.0 copy-start.1
  425.7 0.0 copy-start
  425.8 0.0 copy-start.4
  425.8 0.0 copy-start.3
  425.8 2.1 copy.26
  427.9 2.0 copy.27
  429.9 0.0 copy-done.1
  429.9 0.8 copy.33
  430.7 0.0 copy-done
  430.7 0.8 copy.34
  431.5 0.0 copy-done.4
  431.5 0.5 copy.35
  432.0 0.0 copy-done.3
  432.0 0.7 copy.36
Async XLA Ops:
  0.6 6.1 %copy-start.2 = (f32[1,128,1000]{1,2,0:T(8,128)S(1)}, f32[1,128,1000]{1,2,0:T(8,128)}, u32[]{:S(2)}) copy-start(f32[1,128,1000]{1,2,0:T(8,128)} %param.16) | copy-start | bytes 1536004
  425.7 4.2 copy-start.1
  425.7 5.0 %copy-start = (f32[128,1024]{1,0:T(8,128)S(1)}, f32[128,1024]{1,0:T(8,128)}, u32[]{:S(2)}) copy-start(f32[128,1024]{1,0:T(8,128)} %get-tuple-element.14) | copy-start | bytes 1572868
  425.8 5.8 %copy-start.4 = (f32[1,2]{1,0:T(1,128)S(1)}, f32[1,2]{1,0:T(1,128)}, u32[]{:S(2)}) copy-start(f32[1,2]{1,0:T(1,128)} %get-tuple-element.40) | copy-start | bytes 28
  425.8 6.3 %copy-start.3 = (f32[64,512]{1,0:T(8,128)S(1)}, f32[64,512]{1,0:T(8,128)}, u32[]{:S(2)}) copy-start(f32[64,512]{1,0:T(8,128)} %get-tuple-element.41) | copy-start | bytes 393220

commit v2 on v1

--- a/solution.py
+++ b/solution.py
@@ -89,6 +89,9 @@
 ):
     me = lax.axis_index("dp")
     task = lax.axis_index("task")
+    line = n // 2
+    place, side = me // 2, lax.rem(me, 2)
+    partner = place * 2 + 1 - side
     steps, local_batch, width_in = x_ref.shape
     rows1 = w1_ref.shape[0]
     rows2, class_count = w2_ref.shape
@@ -149,24 +152,14 @@
         )
 
     def one_step(step, carry):
-        def copy(stage, k):
-            peer = lax.rem(me + k, n)
-            if stage == HIDDEN_W:
-                own = full1.at[step, pl.ds(pl.multiple_of(me * rows1, rows1), rows1)]
-                source, target = own, own
-            elif stage == OUT_W:
-                own = full2.at[step, pl.ds(pl.multiple_of(me * rows2, rows2), rows2)]
-                source, target = own, own
-            elif stage == OUT_G:
-                source = send2.at[step, pl.ds(pl.multiple_of(peer * rows2, rows2), rows2)]
-                target = recv2.at[step, k]
-            elif stage == HIDDEN_G:
-                source = send1.at[step, pl.ds(pl.multiple_of(peer * rows1, rows1), rows1)]
-                target = recv1.at[step, k]
-            elif stage == STATS:
+        def small_copy(stage, k):
+            if stage == STATS:
                 source, target = stat_send.at[step], stat_recv.at[step, k]
             else:
                 source, target = share_send.at[step], share_recv.at[step, k]
+            return remote(stage, k, source, target, lax.rem(me + k, n))
+
+        def remote(stage, k, source, target, peer):
             return pltpu.make_async_remote_copy(
                 src_ref=source,
                 dst_ref=target,
@@ -176,22 +169,94 @@
                 device_id_type=MESH,
             )
 
+        def block_of(ref, owner, rows):
+            return ref.at[step, pl.ds(pl.multiple_of(owner * rows, rows), rows)]
+
+        def line_weight(stage, j):
+            full, rows = (full1, rows1) if stage == HIDDEN_W else (full2, rows2)
+            own = block_of(full, me, rows)
+            return remote(stage, j, own, own, lax.rem(place + j, line) * 2 + side)
+
+        def partner_weight(stage, j):
+            full, rows = (full1, rows1) if stage == HIDDEN_W else (full2, rows2)
+            held = block_of(full, lax.rem(place - j + line, line) * 2 + side, rows)
+            return remote(stage, line + j, held, held, partner)
+
+        def partner_grad(stage, j):
+            sent, received, rows = (send2, recv2, rows2) if stage == OUT_G else (send1, recv1, rows1)
+            owner = lax.rem(place + j, line) * 2 + 1 - side
+            return remote(stage, line + j, block_of(sent, owner, rows), received.at[step, line + j], partner)
+
+        def line_grad(stage, j):
+            sent, received, rows = (send2, recv2, rows2) if stage == OUT_G else (send1, recv1, rows1)
+            owner = lax.rem(place + j, line) * 2 + side
+            return remote(stage, j, block_of(sent, owner, rows), received.at[step, j], owner)
+
+        def start_weight(stage):
+            partner_weight(stage, 0).start()
+
+            @pl.loop(1, line)
+            def _(j):
+                line_weight(stage, j).start()
+
+        def forward_weight(stage):
+            @pl.loop(1, line)
+            def _(j):
+                line_weight(stage, j).wait_recv()
+                partner_weight(stage, j).start()
+
+        def arrive_weight(stage):
+            @pl.loop(0, line)
+            def _(j):
+                partner_weight(stage, j).wait_recv()
+
+        def start_grad(stage):
+            @pl.loop(1, line)
+            def _(j):
+                partner_grad(stage, j).start()
+
+            partner_grad(stage, 0).start()
+
+        def forward_grad(stage):
+            sent, received, rows = (send2, recv2, rows2) if stage == OUT_G else (send1, recv1, rows1)
+
+            @pl.loop(1, line)
+            def _(j):
+                partner_grad(stage, j).wait_recv()
+                base = pl.multiple_of((lax.rem(place + j, line) * 2 + side) * rows, rows)
+
+                @pl.loop(0, rows // 16)
+                def _(i):
+                    at = pl.ds(pl.multiple_of(base + i * 16, 16), 16)
+                    other = received[step, line + j, pl.ds(pl.multiple_of(i * 16, 16), 16), :]
+                    both = sent[step, at, :].astype(F32) + other.astype(F32)
+                    sent[step, at, :] = both.astype(BF16)
+
+                line_grad(stage, j).start()
+
+        def arrive_grad(stage):
+            partner_grad(stage, 0).wait_recv()
+
+            @pl.loop(1, line)
+            def _(j):
+                line_grad(stage, j).wait_recv()
+
         def start(stage):
             @pl.loop(1, n)
             def _(k):
-                copy(stage, k).start()
+                small_copy(stage, k).start()
 
         def arrive(stage):
             @pl.loop(1, n)
             def _(k):
-                copy(stage, k).wait_recv()
+                small_copy(stage, k).wait_recv()
 
         full1[step, pl.ds(pl.multiple_of(me * rows1, rows1), rows1)] = p1[...].astype(BF16)
         full2[step, pl.ds(pl.multiple_of(me * rows2, rows2), rows2)] = p2[...].astype(BF16)
-        start(HIDDEN_W)
-        start(OUT_W)
-
-        arrive(HIDDEN_W)
+        start_weight(HIDDEN_W)
+        start_weight(OUT_W)
+        forward_weight(HIDDEN_W)
+        arrive_weight(HIDDEN_W)
 
         @pl.loop(0, local_batch // chunk)
         def _(i):
@@ -199,7 +264,8 @@
             pre = jnp.dot(x_ref[step, at, :], full1[step], preferred_element_type=F32)
             act[at, :] = jnp.maximum(pre * scale_in, 0.0).astype(BF16)
 
-        arrive(OUT_W)
+        forward_weight(OUT_W)
+        arrive_weight(OUT_W)
 
         @pl.loop(0, local_batch // chunk)
         def _(i):
@@ -221,7 +287,7 @@
             grad = lax.dot_general(act[:, at], err[...], BY_ROWS, preferred_element_type=F32)
             send2[step, at, :] = grad.astype(BF16)
 
-        start(OUT_G)
+        start_grad(OUT_G)
 
         @pl.loop(0, local_batch // chunk)
         def _(i):
@@ -236,7 +302,9 @@
             grad = lax.dot_general(x_ref[step, :, at], dpre[...], BY_ROWS, preferred_element_type=F32)
             send1[step, at, :] = grad.astype(BF16)
 
-        start(HIDDEN_G)
+        start_grad(HIDDEN_G)
+        forward_grad(OUT_G)
+        forward_grad(HIDDEN_G)
 
         def reduce(sent, received, gradient, moment, tensor, rows, scale):
             def body(i, sums):
@@ -244,7 +312,7 @@
                 at = pl.ds(offset, 16)
                 own = pl.ds(pl.multiple_of(me * rows + offset, 16), 16)
                 grad = sent[step, own, :].astype(F32)
-                for k in range(1, n):
+                for k in range(1, line + 1):
                     grad = grad + received[step, k, at, :].astype(F32)
                 grad = grad * scale
                 mom = BETA * moment[at, :] + (1.0 - BETA) * grad
@@ -261,9 +329,9 @@
             zero = jnp.zeros((8, LANES), F32)
             return lax.fori_loop(0, rows // 16, body, (zero, zero, zero, zero))
 
-        arrive(OUT_G)
+        arrive_grad(OUT_G)
         sums2 = reduce(send2, recv2, g2, q2, p2, rows2, scale_hidden)
-        arrive(HIDDEN_G)
+        arrive_grad(HIDDEN_G)
         sums1 = reduce(send1, recv1, g1, q1, p1, rows1, scale_in)
         tile = jnp.zeros((8, LANES), F32)
         for row, sums in enumerate((sums1, sums2)):
@@ -356,11 +424,31 @@
         update(p1, g1, q1, 0, width_hidden)
         update(p2, g2, q2, 1, class_count)
 
-        for stage in range(6):
+        for stage in (HIDDEN_W, OUT_W):
+
+            @pl.loop(0, line)
+            def _(j):
+                partner_weight(stage, j).wait_send()
+
+            @pl.loop(1, line)
+            def _(j):
+                line_weight(stage, j).wait_send()
+
+        for stage in (OUT_G, HIDDEN_G):
+
+            @pl.loop(0, line)
+            def _(j):
+                partner_grad(stage, j).wait_send()
+
+            @pl.loop(1, line)
+            def _(j):
+                line_grad(stage, j).wait_send()
+
+        for stage in (STATS, SHARE):
 
             @pl.loop(1, n)
             def _(k):
-                copy(stage, k).wait_send()
+                small_copy(stage, k).wait_send()
 
         return carry
 

time: 433 us -> 279 us (0.64)
  Pallas kernels: 418 us -> 264 us
    pallas_call x1, Pallas kernels: 418 us -> 264 us  [on_device(): pl.pallas_call(functools.partial(kernel, n, tasks), out_shape=out_shape,...]
where the time goes in v2:
time: 279 us; the launch traced here: 278 us
  Pallas kernels  264 us (95%)
  local copies, waits for them, and re-layouts  13.3 us (5%)
    pallas_call x1, Pallas kernels, on_device(): pl.pallas_call(functools.partial(kernel, n, tasks), out_shape=out_shape,...  264 us
    unnamed x19, local copies, waits for them, and re-layouts  11.6 us

profile of v2, /device:TPU:0, one launch (start us, length us, event | category | flops | bytes accessed | tf_op | source)
XLA Modules:
  0.0 278.5 jit_solution(11131151308637124259)
XLA Ops:
  0.6 0.0 copy-start.2
  1.3 1.6 copy.25.hout_ref
  3.0 1.7 copy.24.label_ref
  4.7 2.0 copy.22
  6.7 0.0 copy-done.2
  6.7 1.0 copy.23
  7.7 263.8 %shard_map.154 = (f32[128,1024]{1,0:T(8,128)}, f32[128,1000]{1,0:T(8,128)}, f32[128,1024]{1,0:T(8,128)}, f32[128,1000]{1,0:T(8,128)}, f32[1,2]{1,0:T(1,128)}, /*index=5*/f32[64,512]{1,0:T(8,128)}) custom-call(bf16[2,512,1024]{2,1,0:T(8,128)(2,1)} %bitcast.12, s32[2,512,1]{2,1,0:T(8,128)} %copy.24.label_ref, f32[128,1024]{1,0:T(8,128)} %bitcast.19, ...), custom_call_target="tpu_custom_call" | custom-call | tf_op jit(solution)/shard_map/pallas_call | solution.py:559
  271.5 0.0 copy-start.1
  271.6 0.0 copy-start
  271.6 0.0 copy-start.4
  271.6 0.0 copy-start.3
  271.6 2.1 copy.26
  273.7 2.0 copy.27
  275.7 0.0 copy-done.1
  275.7 0.8 copy.33
  276.5 0.0 copy-done
  276.5 0.8 copy.34
  277.3 0.0 copy-done.4
  277.3 0.5 copy.35
  277.8 0.0 copy-done.3
  277.8 0.7 copy.36
Async XLA Ops:
  0.6 6.1 %copy-start.2 = (f32[1,128,1000]{1,2,0:T(8,128)S(1)}, f32[1,128,1000]{1,2,0:T(8,128)}, u32[]{:S(2)}) copy-start(f32[1,128,1000]{1,2,0:T(8,128)} %param.16) | copy-start | bytes 1536004
  271.5 4.2 %copy-start.1 = (f32[128,1024]{1,0:T(8,128)S(1)}, f32[128,1024]{1,0:T(8,128)}, u32[]{:S(2)}) copy-start(f32[128,1024]{1,0:T(8,128)} %get-tuple-element.12) | copy-start | bytes 1572868
  271.6 5.0 %copy-start = (f32[128,1024]{1,0:T(8,128)S(1)}, f32[128,1024]{1,0:T(8,128)}, u32[]{:S(2)}) copy-start(f32[128,1024]{1,0:T(8,128)} %get-tuple-element.14) | copy-start | bytes 1572868
  271.6 5.8 %copy-start.4 = (f32[1,2]{1,0:T(1,128)S(1)}, f32[1,2]{1,0:T(1,128)}, u32[]{:S(2)}) copy-start(f32[1,2]{1,0:T(1,128)} %get-tuple-element.40) | copy-start | bytes 28
  271.6 6.3 %copy-start.3 = (f32[64,512]{1,0:T(8,128)S(1)}, f32[64,512]{1,0:T(8,128)}, u32[]{:S(2)}) copy-start(f32[64,512]{1,0:T(8,128)} %get-tuple-element.41) | copy-start | bytes 393220
